TPU v7x, 512 devices: a whole 4x4x16 slice. The times are simulated.
512 devices in a mesh: role: 4 (over z_lo), tp: 4 (over x), dp: 32 (over y, z_hi, core).
Axes of the slice: x: 4, y: 4, z: 16 (z_hi: 4, z_lo: 4; z = z_hi * 4 + z_lo), core: 2. Of those that a mesh axis runs over, the one named last changes fastest.
Arguments:
- master: float32 [1024, 8192], P('tp', ('role', 'dp')), may hold values from -0.0625 to 0.0625
- key_bias: float32 [1024], P('tp'), may hold values from -3 to 3
- probe_tokens: bfloat16 [32768, 8192], P(('role', 'dp')), may hold values from -6 to 6
Outputs:
- weight: bfloat16 [8192, 1024], P(None, 'tp')
- probe_keys: bfloat16 [32768, 1024], P(('role', 'dp'), 'tp')
- checksum: float32 [8192], replicated
All inputs are finite; a program needn't handle non-finite values.
Results may differ from a plain program's by a relative error of at most 0.005.
Values may be sent and summed in bfloat16 or wider, within the bound.
No kernel may reach another device: no remote copies, remote signals or barrier semaphores. Data moves between devices by JAX's collectives and lax.ppermute only.
A program may use at most 64 MiB of HBM per device.

v0:
```python
import jax
import jax.numpy as jnp
from jax import lax
from jax.sharding import PartitionSpec as P


def copy_for_each(value, axis):
    copies = jnp.broadcast_to(value, (lax.axis_size(axis), *value.shape))
    return lax.all_to_all(copies, axis, split_axis=0, concat_axis=0, tiled=True)


def over_copies(value, axis):
    return copy_for_each(value, axis).sum(axis=0)


def body(master, key_bias, probe_tokens):
    own_rows = jnp.transpose(master).astype(jnp.bfloat16)
    replica_block = lax.all_gather(own_rows, "dp", axis=0, tiled=True)
    incoming = lax.all_gather(replica_block, "role", axis=0, tiled=True)
    totals = jnp.dot(probe_tokens, incoming, preferred_element_type=jnp.float32)
    probe_keys = (totals + key_bias[None, :]).astype(jnp.bfloat16)
    checksum = over_copies(jnp.sum(incoming.astype(jnp.float32), axis=1), "tp")
    return (incoming, probe_keys, checksum)


def solution(mesh):
    placed = (P("tp", ("role", "dp")), P("tp"), P(("role", "dp"), None))
    return jax.shard_map(
        body,
        mesh=mesh,
        in_specs=placed,
        out_specs=(P(None, "tp"), P(("role", "dp"), "tp"), P()),
        check_vma=False,
    )
```

profile of v0, /device:TPU:2, one launch (start us, length us, event | category | flops | bytes accessed | tf_op | source)
XLA Modules:
  0.0 199.0 jit_solution(13851942847966646415)
XLA Ops:
  7.2 0.0 copy-start
  7.2 0.0 all-gather.3.cloned.1.call-start
  7.2 1.5 convert_bitcast_fusion
  8.7 0.0 all-gather.3.cloned.1.call-update
  8.7 0.0 all-gather.5.cloned.1.call-start
  8.8 79.2 %all-gather.3.cloned.1.call-done = bf16[2048,256]{1,0:T(8,128)(2,1)} async-done(((bf16[64,256]{1,0:T(8,128)(2,1)}), bf16[2048,256]{1,0:T(8,128)(2,1)}) %all-gather.3.cloned.1.call-update) | async-done | bytes 1048592 | tf_op jit(solution)/shard_map/all_gather | solution.py:18
  87.9 0.0 all-gather.5.cloned.1.call-update
  88.0 84.8 %all-gather.5.cloned.1.call-done = bf16[8192,256]{1,0:T(8,128)(2,1)} async-done(((bf16[2048,256]{1,0:T(8,128)(2,1)}), bf16[8192,256]{1,0:T(8,128)(2,1)}) %all-gather.5.cloned.1.call-update) | async-done | bytes 4194320 | tf_op jit(solution)/shard_map/all_gather | solution.py:19
  172.7 3.3 %convert_reduce_fusion = f32[8192]{0:T(1024)S(1)} fusion(bf16[8192,256]{1,0:T(8,128)(2,1)} %all-gather.5.cloned.1.call-done), kind=kLoop, calls=%fused_computation | loop fusion | flops 4186112 | bytes 4227072 | tf_op jit(solution)/shard_map/reduce_sum | solution.py:22
  176.1 0.7 broadcast_in_dim.4
  176.8 4.8 %all-to-all-start = ((f32[4,1,8192]{2,1,0:T(1,128)}), f32[4,1,8192]{2,1,0:T(1,128)S(1)}, u32[]{:S(2)}, u32[]{:S(2)}) async-start(f32[4,1,8192]{2,1,0:T(1,128)} %broadcast_in_dim.4), calls=%async_computation | async-start | bytes 262144 | tf_op jit(solution)/shard_map/all_to_all | solution.py:9
  181.6 0.0 copy-done
  181.6 5.4 %fusion = bf16[256,256]{1,0:T(8,128)(2,1)} fusion(bf16[256,8192]{1,0:T(8,128)(2,1)} %param.5, bf16[8192,256]{1,0:T(8,128)(2,1)} %all-gather.5.cloned.1.call-done, f32[256]{0:T(256)S(1)} %copy-done), kind=kOutput, calls=%fused_computation.2 | convolution fusion | flops 1073872896 | bytes 8520704 | tf_op jit(solution)/shard_map/dot_general | solution.py:20
  187.0 0.0 all-to-all-done
  187.0 0.7 reduce_sum.19
  187.7 4.5 %copy.9 = bf16[8192,256]{1,0:T(8,128)(2,1)} copy(bf16[8192,256]{1,0:T(8,128)(2,1)} %all-gather.5.cloned.1.call-done) | data formatting | bytes 8388608
Async XLA Ops:
  7.2 174.4 %copy-start = (f32[256]{0:T(256)S(1)}, f32[256]{0:T(256)}, u32[]{:S(2)}) copy-start(f32[256]{0:T(256)} %param.4) | copy-start | bytes 3076
  7.2 80.8 %all-gather.3.cloned.1.call-start = ((), (), s32[]{:S(2)}) async-start(), calls=%async_computation.1 | async-start | bytes 1081344 | tf_op jit(solution)/shard_map/all_gather | solution.py:18
  8.7 164.0 %all-gather.5.cloned.1.call-start = ((), (), s32[]{:S(2)}) async-start(), calls=%async_computation.2 | async-start | bytes 5242880 | tf_op jit(solution)/shard_map/all_gather | solution.py:19
  176.8 10.2 %all-to-all-start = ((f32[4,1,8192]{2,1,0:T(1,128)}), f32[4,1,8192]{2,1,0:T(1,128)S(1)}, u32[]{:S(2)}, u32[]{:S(2)}) async-start(f32[4,1,8192]{2,1,0:T(1,128)} %broadcast_in_dim.4), calls=%async_computation | async-start | bytes 262144 | tf_op jit(solution)/shard_map/all_to_all | solution.py:9
Sparse Core Ops, SparseCore 0:
  11.7 76.1 all-gather.2
  90.0 82.6 all-gather.4
where the time goes:
time: 199 us
  waiting for transfers between devices  164 us (82%)
  between operations  14.1 us (7%)
  other arithmetic  5.54 us (3%)
  matrix products  5.37 us (3%)
  local copies, waits for them, and re-layouts  5.2 us (3%)
  starting transfers between devices  4.88 us (2%)
    all_gather x1, waiting for transfers between devices, body(): incoming = lax.all_gather(replica_block, 'role', axis=0, tiled=True)  84.8 us
    all_gather x1, waiting for transfers between devices, body(): replica_block = lax.all_gather(own_rows, 'dp', axis=0, tiled=True)  79.2 us
    dot_general x1, matrix products, body(): totals = jnp.dot(probe_tokens, incoming, preferred_element_type=jnp.float32)  5.37 us
    all_to_all x1, starting transfers between devices, copy_for_each(): return lax.all_to_all(copies, axis, split_axis=0, concat_axis=0, tiled=True)  4.8 us
    unnamed x3, local copies, waits for them, and re-layouts  4.47 us
  transfers between devices with their start and end apart: 3, of which 2 were waited for; matrix products, arithmetic and copies ran while one was open for 3% of the time, Pallas kernels for 0%

commit v1 on v0

--- a/solution.py
+++ b/solution.py
@@ -16,7 +16,9 @@
 def body(master, key_bias, probe_tokens):
     own_rows = jnp.transpose(master).astype(jnp.bfloat16)
     replica_block = lax.all_gather(own_rows, "dp", axis=0, tiled=True)
-    incoming = lax.all_gather(replica_block, "role", axis=0, tiled=True)
+    incoming = jnp.concatenate(
+        lax.all_to_all(jnp.stack([replica_block] * lax.axis_size("role")), "role", 0, 0), axis=0
+    )
     totals = jnp.dot(probe_tokens, incoming, preferred_element_type=jnp.float32)
     probe_keys = (totals + key_bias[None, :]).astype(jnp.bfloat16)
     checksum = over_copies(jnp.sum(incoming.astype(jnp.float32), axis=1), "tp")

time: 199 us -> 212 us (1.065)
  blocking collectives: 0 us -> 96.4 us
  waiting for transfers between devices: 164 us -> 79.2 us
  local copies, waits for them, and re-layouts: 5.2 us -> 8.63 us
  other arithmetic: 5.54 us -> 3.37 us
    all_to_all x0 -> x1, blocking collectives: none -> 96.4 us  [body(): lax.all_to_all(jnp.stack([replica_block] * lax.axis_size('role')), 'role'...]
    all_gather x1 -> x0, waiting for transfers between devices: 84.8 us -> none  [body(): incoming = lax.all_gather(replica_block, 'role', axis=0, tiled=True)]
    reduce_sum x1, other arithmetic: 3.34 us -> 1.17 us  [body(): checksum = over_copies(jnp.sum(incoming.astype(jnp.float32), axis=1), 'tp')]
    unnamed x3 -> x6, local copies, waits for them, and re-layouts: 4.47 us -> 6.41 us
  transfers between devices with their start and end apart: 3 -> 2, of which waited for: 2 -> 1; matrix products, arithmetic and copies ran while one was open for 3% -> 3% of each run, Pallas kernels for 0% -> 0%
where the time goes in v1:
time: 212 us
  blocking collectives  96.4 us (45%)
  waiting for transfers between devices  79.2 us (37%)
  between operations  14 us (7%)
  local copies, waits for them, and re-layouts  8.63 us (4%)
  matrix products  5.37 us (3%)
  starting transfers between devices  4.84 us (2%)
  other arithmetic  3.37 us (2%)
    all_to_all x1, blocking collectives, body(): lax.all_to_all(jnp.stack([replica_block] * lax.axis_size('role')), 'role'...  96.4 us
    all_gather x1, waiting for transfers between devices, body(): replica_block = lax.all_gather(own_rows, 'dp', axis=0, tiled=True)  79.2 us
    unnamed x6, local copies, waits for them, and re-layouts  6.41 us
    dot_general x1, matrix products, body(): totals = jnp.dot(probe_tokens, incoming, preferred_element_type=jnp.float32)  5.37 us
    all_to_all x1, starting transfers between devices, copy_for_each(): return lax.all_to_all(copies, axis, split_axis=0, concat_axis=0, tiled=True)  4.8 us
  transfers between devices with their start and end apart: 2, of which 1 were waited for; matrix products, arithmetic and copies ran while one was open for 3% of the time, Pallas kernels for 0%

profile of v1, /device:TPU:2, one launch (start us, length us, event | category | flops | bytes accessed | tf_op | source)
XLA Modules:
  0.0 211.9 jit_solution(2521690471913628261)
XLA Ops:
  7.2 0.0 all-gather.2.cloned.1.call-start
  7.2 1.5 convert_bitcast_fusion
  8.7 0.0 all-gather.2.cloned.1.call-update
  8.7 79.2 %all-gather.2.cloned.1.call-done = bf16[2048,256]{1,0:T(8,128)(2,1)} async-done(((bf16[64,256]{1,0:T(8,128)(2,1)}), bf16[2048,256]{1,0:T(8,128)(2,1)}) %all-gather.2.cloned.1.call-update) | async-done | bytes 1048592 | tf_op jit(solution)/shard_map/all_gather | solution.py:18
  87.9 1.5 stack.2
  89.4 96.4 %all_to_all.11 = bf16[4,2048,256]{2,1,0:T(8,128)(2,1)S(1)} all-to-all(bf16[4,2048,256]{2,1,0:T(8,128)(2,1)S(1)} %stack.2), channel_id=1, replica_groups=mesh['role'=4,'tp'=4,'dp'=32] {'role'}, dimensions={0} | all-to-all | bytes 8388608 | tf_op jit(solution)/shard_map/all_to_all | solution.py:20
  185.8 0.0 copy-start
  185.8 1.9 copy-done
  187.7 0.0 copy-start.1
  187.7 1.2 convert_reduce_fusion
  188.9 0.7 broadcast_in_dim.7
  189.6 4.8 %all-to-all-start.1 = ((f32[4,1,8192]{2,1,0:T(1,128)}), f32[4,1,8192]{2,1,0:T(1,128)S(1)}, u32[]{:S(2)}, u32[]{:S(2)}) async-start(f32[4,1,8192]{2,1,0:T(1,128)} %broadcast_in_dim.7), calls=%async_computation.1 | async-start | bytes 262144 | tf_op jit(solution)/shard_map/all_to_all | solution.py:9
  194.4 0.0 copy-done.1
  194.4 5.4 %fusion = bf16[256,256]{1,0:T(8,128)(2,1)} fusion(bf16[256,8192]{1,0:T(8,128)(2,1)} %param.5, bf16[8192,256]{1,0:T(8,128)(2,1)} %bitcast.7, f32[256]{0:T(256)S(1)} %copy-done.1), kind=kOutput, calls=%fused_computation.2 | convolution fusion | flops 1073872896 | bytes 8520704 | tf_op jit(solution)/shard_map/dot_general | solution.py:22
  199.8 0.0 all-to-all-done.1
  199.8 0.7 reduce_sum.19
  200.6 4.5 %copy.10 = bf16[8192,256]{1,0:T(8,128)(2,1)} copy(bf16[8192,256]{1,0:T(8,128)(2,1)} %bitcast.8) | data formatting | bytes 8388608
  (1 shorter events, 0.0 us)
Async XLA Ops:
  7.2 80.8 %all-gather.2.cloned.1.call-start = ((), (), s32[]{:S(2)}) async-start(), calls=%async_computation.2 | async-start | bytes 1081344 | tf_op jit(solution)/shard_map/all_gather | solution.py:18
  185.8 1.9 copy-start
  187.7 6.7 %copy-start.1 = (f32[256]{0:T(256)S(1)}, f32[256]{0:T(256)}, u32[]{:S(2)}) copy-start(f32[256]{0:T(256)} %param.4) | copy-start | bytes 3076
  189.6 10.2 %all-to-all-start.1 = ((f32[4,1,8192]{2,1,0:T(1,128)}), f32[4,1,8192]{2,1,0:T(1,128)S(1)}, u32[]{:S(2)}, u32[]{:S(2)}) async-start(f32[4,1,8192]{2,1,0:T(1,128)} %broadcast_in_dim.7), calls=%async_computation.1 | async-start | bytes 262144 | tf_op jit(solution)/shard_map/all_to_all | solution.py:9
Sparse Core Ops, SparseCore 0:
  11.7 76.1 all-gather.1
